TPU v7x, 32 devices: a whole 2x2x4 slice. The times are simulated.
32 devices in a mesh: dp: 16 (over z, x, core), tp: 2 (over y).
Axes of the slice: x: 2, y: 2, z: 4, core: 2. Of those that a mesh axis runs over, the one named last changes fastest.
Arguments:
- stash_values: bfloat16 [4096, 8192], P(('dp', 'tp')), may hold values from -127 to 127
- stash_scales: bfloat16 [4096, 64], P(('dp', 'tp')), may hold values from 0.001 to 0.13
- value_grad: bfloat16 [4096, 256], P('dp', 'tp'), may hold values from -19 to 19
Outputs:
- clipped_grad: float32 [8192, 256], P('dp', 'tp')
All inputs are finite; a program needn't handle non-finite values.
Results may differ from a plain program's by a relative error of at most 0.0019.
Values may be sent and summed in bfloat16 or wider, within the bound.
No kernel may reach another device: no remote copies, remote signals or barrier semaphores. Data moves between devices by JAX's collectives and lax.ppermute only.
A program may use at most 64 MiB of HBM per device.

v0:
```python
import jax
import jax.numpy as jnp
from jax import lax
from jax.sharding import PartitionSpec as P


def block_dequantize(values, scales):
    rows = values.shape[0]
    blocks = scales.shape[1]
    scaled = (
        values.astype(jnp.float32).reshape(rows, blocks, values.shape[1] // blocks)
        * scales.astype(jnp.float32)[:, :, None]
    )
    return scaled.reshape(rows, values.shape[1]).astype(jnp.bfloat16)


def body(stash_values, stash_scales, value_grad):
    width = stash_values.shape[1]
    columns = value_grad.shape[1]
    dp_count = lax.axis_size("dp")
    tp_count = lax.axis_size("tp")
    own_tokens = stash_values.shape[0]
    sub_rows = width // (dp_count * tp_count)
    inputs = block_dequantize(stash_values, stash_scales)
    inputs = inputs.reshape(own_tokens, dp_count, tp_count, sub_rows)
    features = lax.all_to_all(inputs, "tp", split_axis=2, concat_axis=0, tiled=True)
    features = features.reshape(own_tokens * tp_count, dp_count * sub_rows)
    all_heads = lax.dot_general(
        features,
        lax.all_gather(value_grad, "tp", axis=1, tiled=True),
        (((0,), (0,)), ((), ())),
        preferred_element_type=jnp.float32,
    )
    summed = lax.psum_scatter(all_heads, "dp", scatter_dimension=0, tiled=True)
    local = lax.all_to_all(summed, "tp", split_axis=1, concat_axis=0, tiled=True)
    total = lax.psum(jnp.sum(summed * summed), ("dp", "tp"))
    limit = jnp.sqrt(jnp.float32(width * columns * lax.axis_size("tp")))
    return local * jnp.minimum(jnp.float32(1.0), limit / jnp.sqrt(total))


def solution(mesh):
    placed = (P(("dp", "tp"), None), P(("dp", "tp"), None), P("dp", "tp"))
    return jax.shard_map(body, mesh=mesh, in_specs=placed, out_specs=P("dp", "tp"), check_vma=False)
```

profile of v0, /device:TPU:0, one launch (start us, length us, event | category | flops | bytes accessed | tf_op | source)
XLA Modules:
  0.0 181.6 jit_solution(3500669515704277287)
XLA Ops:
  6.5 0.8 copy.9
  7.3 0.0 copy-start
  7.4 1.1 mul.26
  8.5 0.4 copy-done
  8.9 3.8 %fusion = bf16[128,8192]{1,0:T(8,128)(2,1)} fusion(f32[16,8,64,128]{3,2,1,0:T(8,128)S(1)} %bitcast.22, bf16[128,8192]{1,0:T(8,128)(2,1)S(1)} %copy-done), kind=kLoop, calls=%fused_computation.1 | loop fusion | flops 3145728 | bytes 8388608 | tf_op jit(solution)/shard_map/convert_element_type | solution.py:14
  12.7 3.3 %reshape.16 = bf16[128,16,2,256]{3,2,1,0:T(2,128)(2,1)S(1)} reshape(bf16[128,8192]{1,0:T(8,128)(2,1)} %fusion) | data formatting | bytes 4194304 | tf_op jit(solution)/shard_map/reshape | solution.py:25
  16.0 1.7 copy.10
  17.7 0.0 copy-start.1
  17.7 4.4 %all-to-all-start = ((bf16[128,16,2,256]{3,1,0,2:T(8,128)(2,1)}), bf16[128,16,2,256]{3,1,0,2:T(8,128)(2,1)S(1)}, u32[]{:S(2)}, u32[]{:S(2)}) async-start(bf16[128,16,2,256]{3,1,0,2:T(8,128)(2,1)} %copy.10), calls=%async_computation | async-start | bytes 4194304 | tf_op jit(solution)/shard_map/all_to_all | solution.py:26
  22.1 0.0 reduce-scatter.2.cloned.1.call-start
  22.1 0.0 copy-done.1
  22.1 27.3 %all_gather.3 = bf16[256,256]{1,0:T(8,128)(2,1)S(1)} all-gather(bf16[256,128]{1,0:T(8,128)(2,1)S(1)} %copy-done.1), channel_id=1, replica_groups=mesh['dp'=16,'tp'=2] {'tp'}, dimensions={1}, use_global_device_ids=true | all-gather | bytes 196608 | tf_op jit(solution)/shard_map/all_gather | solution.py:30
  49.4 0.0 all-to-all-done
  49.4 0.9 copy.14
  50.3 2.7 %fusion.1 = f32[4096,256]{1,0:T(8,128)} fusion(bf16[256,4096]{1,0:T(8,128)(2,1)S(1)} %bitcast.23, bf16[256,256]{1,0:T(8,128)(2,1)S(1)} %all_gather.3), kind=kOutput, calls=%fused_computation.5 | convolution fusion | flops 536870912 | bytes 6422528 | tf_op jit(solution)/shard_map/dot_general | solution.py:28
  53.0 0.0 reduce-scatter.2.cloned.1.call-update
  53.1 73.4 %reduce-scatter.2.cloned.1.call-done = f32[256,256]{1,0:T(8,128)} async-done(((f32[4096,256]{1,0:T(8,128)}), f32[256,256]{1,0:T(8,128)}) %reduce-scatter.2.cloned.1.call-update) | async-done | bytes 262160 | tf_op jit(solution)/shard_map/reduce_scatter | solution.py:34
  126.5 1.7 copy_bitcast_fusion
  128.2 3.4 %all-to-all-start.1 = ((f32[256,2,128]{2,0,1:T(8,128)}), f32[256,2,128]{2,0,1:T(8,128)S(1)}, u32[]{:S(2)}, u32[]{:S(2)}) async-start(f32[256,2,128]{2,0,1:T(8,128)} %copy_bitcast_fusion), calls=%async_computation.2 | async-start | bytes 524288 | tf_op jit(solution)/shard_map/all_to_all | solution.py:35
  131.6 1.6 multiply_reduce_fusion
  133.2 40.2 %psum.7 = f32[]{:T(128)} all-reduce(f32[]{:T(128)} %multiply_reduce_fusion), channel_id=1, replica_groups=mesh['dp'=16,'tp'=2] {'dp','tp'}, use_global_device_ids=true, to_apply=%region_2.0 | all-reduce | flops 1 | bytes 8 | tf_op jit(solution)/shard_map/psum | solution.py:36
  174.0 0.0 all-to-all-done.1
  174.1 0.7 broadcast_multiply_fusion
Async XLA Ops:
  7.3 1.6 copy-start
  17.7 4.4 %copy-start.1 = (bf16[256,128]{1,0:T(8,128)(2,1)S(1)}, bf16[256,128]{1,0:T(8,128)(2,1)}, u32[]{:S(2)}) copy-start(bf16[256,128]{1,0:T(8,128)(2,1)} %param.5) | copy-start | bytes 196612
  17.7 31.7 %all-to-all-start = ((bf16[128,16,2,256]{3,1,0,2:T(8,128)(2,1)}), bf16[128,16,2,256]{3,1,0,2:T(8,128)(2,1)S(1)}, u32[]{:S(2)}, u32[]{:S(2)}) async-start(bf16[128,16,2,256]{3,1,0,2:T(8,128)(2,1)} %copy.10), calls=%async_computation | async-start | bytes 4194304 | tf_op jit(solution)/shard_map/all_to_all | solution.py:26
  22.1 104.4 %reduce-scatter.2.cloned.1.call-start = ((), (), s32[]{:S(2)}) async-start(), calls=%async_computation.3 | async-start | bytes 4456448 | tf_op jit(solution)/shard_map/reduce_scatter | solution.py:34
  128.2 45.9 %all-to-all-start.1 = ((f32[256,2,128]{2,0,1:T(8,128)}), f32[256,2,128]{2,0,1:T(8,128)S(1)}, u32[]{:S(2)}, u32[]{:S(2)}) async-start(f32[256,2,128]{2,0,1:T(8,128)} %copy_bitcast_fusion), calls=%async_computation.2 | async-start | bytes 524288 | tf_op jit(solution)/shard_map/all_to_all | solution.py:35
Sparse Core Ops, SparseCore 0:
  53.2 73.2 reduce-scatter.1
where the time goes:
time: 182 us
  waiting for transfers between devices  73.4 us (40%)
  blocking collectives  67.5 us (37%)
  between operations  14 us (8%)
  local copies, waits for them, and re-layouts  9.97 us (5%)
  starting transfers between devices  7.84 us (4%)
  other arithmetic  6.12 us (3%)
  matrix products  2.71 us (1%)
    reduce_scatter x1, waiting for transfers between devices, body(): summed = lax.psum_scatter(all_heads, 'dp', scatter_dimension=0, tiled=True)  73.4 us
    psum x1, blocking collectives, body(): total = lax.psum(jnp.sum(summed * summed), ('dp', 'tp'))  40.2 us
    all_gather x1, blocking collectives, body(): lax.all_gather(value_grad, 'tp', axis=1, tiled=True)  27.3 us
    reshape x2, local copies, waits for them, and re-layouts, body(): inputs = inputs.reshape(own_tokens, dp_count, tp_count, sub_rows)  4.97 us
    all_to_all x1, starting transfers between devices, body(): lax.all_to_all(inputs, 'tp', split_axis=2, concat_axis=0, tiled=True)  4.39 us
    convert_element_type x1, other arithmetic, block_dequantize(): return scaled.reshape(rows, values.shape[1]).astype(jnp.bfloat16)  3.79 us
  transfers between devices with their start and end apart: 3, of which 1 were waited for; matrix products, arithmetic and copies ran while one was open for 1% of the time, Pallas kernels for 0%

commit v1 on v0

--- a/solution.py
+++ b/solution.py
@@ -27,7 +27,9 @@
     features = features.reshape(own_tokens * tp_count, dp_count * sub_rows)
     all_heads = lax.dot_general(
         features,
-        lax.all_gather(value_grad, "tp", axis=1, tiled=True),
+        jnp.concatenate(
+            lax.all_to_all(jnp.stack([value_grad] * lax.axis_size("tp")), "tp", 0, 0), axis=1
+        ),
         (((0,), (0,)), ((), ())),
         preferred_element_type=jnp.float32,
     )

time: 182 us -> 188 us (1.033)
  blocking collectives: 67.5 us -> 40.2 us
  waiting for transfers between devices: 73.4 us -> 100 us
  starting transfers between devices: 7.84 us -> 11.3 us
    all_gather x1 -> x0, blocking collectives: 27.3 us -> none  [body(): lax.all_gather(value_grad, 'tp', axis=1, tiled=True)]
    all_to_all x1, waiting for transfers between devices: 0.01 us -> 25.1 us  [body(): lax.all_to_all(inputs, 'tp', split_axis=2, concat_axis=0, tiled=True)]
    all_to_all x0 -> x1, starting transfers between devices: none -> 3.38 us  [body(): lax.all_to_all(jnp.stack([value_grad] * lax.axis_size('tp')), 'tp', 0, 0)]
  transfers between devices with their start and end apart: 3 -> 4, of which waited for: 1 -> 3; matrix products, arithmetic and copies ran while one was open for 1% -> 3% of each run, Pallas kernels for 0% -> 0%
where the time goes in v1:
time: 188 us; the launch traced here: 187 us
  waiting for transfers between devices  100 us (53%)
  blocking collectives  40.2 us (21%)
  between operations  14.1 us (8%)
  local copies, waits for them, and re-layouts  11.7 us (6%)
  starting transfers between devices  11.3 us (6%)
  other arithmetic  6.81 us (4%)
  matrix products  2.71 us (1%)
    reduce_scatter x1, waiting for transfers between devices, body(): summed = lax.psum_scatter(all_heads, 'dp', scatter_dimension=0, tiled=True)  73.4 us
    psum x1, blocking collectives, body(): total = lax.psum(jnp.sum(summed * summed), ('dp', 'tp'))  40.2 us
    all_to_all x1, waiting for transfers between devices, body(): lax.all_to_all(inputs, 'tp', split_axis=2, concat_axis=0, tiled=True)  25.1 us
    reshape x2, local copies, waits for them, and re-layouts, body(): inputs = inputs.reshape(own_tokens, dp_count, tp_count, sub_rows)  4.96 us
    all_to_all x1, starting transfers between devices, body(): lax.all_to_all(inputs, 'tp', split_axis=2, concat_axis=0, tiled=True)  4.39 us
    convert_element_type x1, other arithmetic, block_dequantize(): return scaled.reshape(rows, values.shape[1]).astype(jnp.bfloat16)  3.77 us
  transfers between devices with their start and end apart: 4, of which 3 were waited for; matrix products, arithmetic and copies ran while one was open for 3% of the time, Pallas kernels for 0%

profile of v1, /device:TPU:0, one launch (start us, length us, event | category | flops | bytes accessed | tf_op | source)
XLA Modules:
  0.0 187.2 jit_solution(955448882181115075)
XLA Ops:
  6.5 0.8 copy.10
  7.3 0.0 copy-start.1
  7.4 1.1 mul.26
  8.5 0.4 copy-done.1
  8.9 3.8 %fusion = bf16[128,8192]{1,0:T(8,128)(2,1)} fusion(f32[16,8,64,128]{3,2,1,0:T(8,128)S(1)} %bitcast.26, bf16[128,8192]{1,0:T(8,128)(2,1)S(1)} %copy-done.1), kind=kLoop, calls=%fused_computation.1 | loop fusion | flops 3145728 | bytes 8388608 | tf_op jit(solution)/shard_map/convert_element_type | solution.py:14
  12.7 3.3 %reshape.22 = bf16[128,16,2,256]{3,2,1,0:T(2,128)(2,1)S(1)} reshape(bf16[128,8192]{1,0:T(8,128)(2,1)} %fusion) | data formatting | bytes 4194304 | tf_op jit(solution)/shard_map/reshape | solution.py:25
  16.0 1.7 copy.11
  17.7 0.0 copy-start.2
  17.7 4.4 %all-to-all-start = ((bf16[128,16,2,256]{3,1,0,2:T(8,128)(2,1)}), bf16[128,16,2,256]{3,1,0,2:T(8,128)(2,1)S(1)}, u32[]{:S(2)}, u32[]{:S(2)}) async-start(bf16[128,16,2,256]{3,1,0,2:T(8,128)(2,1)} %copy.11), calls=%async_computation | async-start | bytes 4194304 | tf_op jit(solution)/shard_map/all_to_all | solution.py:26
  22.1 0.0 copy-done.2
  22.1 0.1 copy.12
  22.2 0.7 pad_maximum_fusion
  22.9 25.1 %all-to-all-done = bf16[128,16,2,256]{3,1,0,2:T(8,128)(2,1)S(1)} async-done(((bf16[128,16,2,256]{3,1,0,2:T(8,128)(2,1)}), bf16[128,16,2,256]{3,1,0,2:T(8,128)(2,1)S(1)}, u32[]{:S(2)}, u32[]{:S(2)}) %all-to-all-start) | async-done | bytes 2097184 | tf_op jit(solution)/shard_map/all_to_all | solution.py:26
  47.9 0.0 copy-start
  47.9 3.4 %all-to-all-start.1 = ((bf16[2,256,128]{1,2,0:T(8,128)(2,1)}), bf16[2,256,128]{1,2,0:T(8,128)(2,1)S(1)}, u32[]{:S(2)}, u32[]{:S(2)}) async-start(bf16[2,256,128]{1,2,0:T(8,128)(2,1)} %pad_maximum_fusion), calls=%async_computation.1 | async-start | bytes 262144 | tf_op jit(solution)/shard_map/all_to_all | solution.py:31
  51.3 0.0 reduce-scatter.2.cloned.1.call-start
  51.4 0.0 copy-done
  51.4 2.5 %copy.16 = bf16[32,8,16,256]{3,1,2,0:T(8,128)(2,1)S(1)} copy(bf16[32,8,16,256]{3,2,1,0:T(8,128)(2,1)} %bitcast.28) | data formatting | bytes 4194304
  53.9 1.9 all-to-all-done.1
  55.8 2.7 %fusion.1 = f32[4096,256]{1,0:T(8,128)} fusion(bf16[256,4096]{1,0:T(8,128)(2,1)S(1)} %bitcast.27, bf16[256,256]{0,1:T(8,128)(2,1)S(1)} %bitcast.29), kind=kOutput, calls=%fused_computation.6 | convolution fusion | flops 536870912 | bytes 6422528 | tf_op jit(solution)/shard_map/dot_general | solution.py:28
  58.5 0.0 reduce-scatter.2.cloned.1.call-update
  58.5 73.4 %reduce-scatter.2.cloned.1.call-done = f32[256,256]{1,0:T(8,128)} async-done(((f32[4096,256]{1,0:T(8,128)}), f32[256,256]{1,0:T(8,128)}) %reduce-scatter.2.cloned.1.call-update) | async-done | bytes 262160 | tf_op jit(solution)/shard_map/reduce_scatter | solution.py:36
  131.9 1.7 copy_bitcast_fusion
  133.6 3.4 %all-to-all-start.2 = ((f32[256,2,128]{2,0,1:T(8,128)}), f32[256,2,128]{2,0,1:T(8,128)S(1)}, u32[]{:S(2)}, u32[]{:S(2)}) async-start(f32[256,2,128]{2,0,1:T(8,128)} %copy_bitcast_fusion), calls=%async_computation.3 | async-start | bytes 524288 | tf_op jit(solution)/shard_map/all_to_all | solution.py:37
  137.1 1.7 multiply_reduce_fusion
  138.7 40.2 %psum.7 = f32[]{:T(128)} all-reduce(f32[]{:T(128)} %multiply_reduce_fusion), channel_id=1, replica_groups=mesh['dp'=16,'tp'=2] {'dp','tp'}, use_global_device_ids=true, to_apply=%region_2.0 | all-reduce | flops 1 | bytes 8 | tf_op jit(solution)/shard_map/psum | solution.py:38
  179.6 0.0 all-to-all-done.2
  179.6 0.7 broadcast_multiply_fusion
Async XLA Ops:
  7.3 1.6 copy-start.1
  17.7 4.4 %copy-start.2 = (bf16[256,128]{1,0:T(8,128)(2,1)S(1)}, bf16[256,128]{1,0:T(8,128)(2,1)}, u32[]{:S(2)}) copy-start(bf16[256,128]{1,0:T(8,128)(2,1)} %param.5) | copy-start | bytes 196612
  17.7 30.2 %all-to-all-start = ((bf16[128,16,2,256]{3,1,0,2:T(8,128)(2,1)}), bf16[128,16,2,256]{3,1,0,2:T(8,128)(2,1)S(1)}, u32[]{:S(2)}, u32[]{:S(2)}) async-start(bf16[128,16,2,256]{3,1,0,2:T(8,128)(2,1)} %copy.11), calls=%async_computation | async-start | bytes 4194304 | tf_op jit(solution)/shard_map/all_to_all | solution.py:26
  47.9 3.4 %copy-start = (bf16[128,16,2,256]{3,1,0,2:T(8,128)(2,1)}, bf16[128,16,2,256]{3,1,0,2:T(8,128)(2,1)S(1)}, u32[]{:S(2)}) copy-start(bf16[128,16,2,256]{3,1,0,2:T(8,128)(2,1)S(1)} %all-to-all-done) | copy-start | bytes 6291460
  47.9 7.8 %all-to-all-start.1 = ((bf16[2,256,128]{1,2,0:T(8,128)(2,1)}), bf16[2,256,128]{1,2,0:T(8,128)(2,1)S(1)}, u32[]{:S(2)}, u32[]{:S(2)}) async-start(bf16[2,256,128]{1,2,0:T(8,128)(2,1)} %pad_maximum_fusion), calls=%async_computation.1 | async-start | bytes 262144 | tf_op jit(solution)/shard_map/all_to_all | solution.py:31
  51.3 80.6 %reduce-scatter.2.cloned.1.call-start = ((), (), s32[]{:S(2)}) async-start(), calls=%async_computation.4 | async-start | bytes 4456448 | tf_op jit(solution)/shard_map/reduce_scatter | solution.py:36
  133.6 46.0 %all-to-all-start.2 = ((f32[256,2,128]{2,0,1:T(8,128)}), f32[256,2,128]{2,0,1:T(8,128)S(1)}, u32[]{:S(2)}, u32[]{:S(2)}) async-start(f32[256,2,128]{2,0,1:T(8,128)} %copy_bitcast_fusion), calls=%async_computation.3 | async-start | bytes 524288 | tf_op jit(solution)/shard_map/all_to_all | solution.py:37
Sparse Core Ops, SparseCore 0:
  58.6 73.2 reduce-scatter.1
